TPU v7x, 128 devices: a whole 4x4x4 slice. The times are simulated.
128 devices in a mesh: dp: 16 (over x_hi, z, core), blk: 8 (over y, x_lo).
Axes of the slice: x: 4 (x_hi: 2, x_lo: 2; x = x_hi * 2 + x_lo), y: 4, z: 4, core: 2. Of those that a mesh axis runs over, the one named last changes fastest.
Arguments:
- inputs: bfloat16 [512, 8192], P('blk', 'dp'), may hold values from -6 to 6
- upstream: bfloat16 [512, 8192], P('blk', 'dp'), may hold values from -1.5 to 1.5
- gate_weight: bfloat16 [8192, 14784], P('dp', 'blk'), may hold values from -0.0625 to 0.0625
- up_weight: bfloat16 [8192, 14784], P('dp', 'blk'), may hold values from -0.0625 to 0.0625
- down_weight: bfloat16 [14784, 8192], P('blk', 'dp'), may hold values from -0.046875 to 0.046875
Outputs:
- input_grad: bfloat16 [512, 8192], P('blk', 'dp')
- gate_grad: bfloat16 [8192, 14784], P('dp', 'blk')
- up_grad: bfloat16 [8192, 14784], P('dp', 'blk')
- down_grad: bfloat16 [14784, 8192], P('blk', 'dp')
All inputs are finite; a program needn't handle non-finite values.
Results may differ from a plain program's by a relative error of at most 0.005.
Values may be sent and summed in bfloat16 or wider, within the bound.
A program may use at most 128 MiB of HBM per device.

v0:
```python
import jax
import jax.numpy as jnp
from jax import lax
from jax.sharding import PartitionSpec as P


def contract_last(left, right):
    return lax.dot_general(
        left, right, (((1,), (1,)), ((), ())), preferred_element_type=jnp.float32
    )


def contract_first(left, right):
    return lax.dot_general(
        left, right, (((0,), (0,)), ((), ())), preferred_element_type=jnp.float32
    )


def elementwise(gate, up, back):
    sig = jax.nn.sigmoid(gate)
    hidden = (gate * sig * up).astype(jnp.bfloat16)
    up_delta = (back * gate * sig).astype(jnp.bfloat16)
    gate_delta = (back * up * sig * (1.0 + gate * (1.0 - sig))).astype(jnp.bfloat16)
    return (hidden, gate_delta, up_delta)


def local(inputs, upstream, gate_weight, up_weight, down_weight):
    both = lax.all_gather(jnp.concatenate([inputs, upstream], 1), "blk", axis=0, tiled=True)
    width = inputs.shape[1]
    rows_all, grads_all = (both[:, :width], both[:, width:])
    parts = [
        jnp.dot(rows_all, gate_weight, preferred_element_type=jnp.float32),
        jnp.dot(rows_all, up_weight, preferred_element_type=jnp.float32),
        contract_last(grads_all, down_weight),
    ]
    sums = [lax.psum_scatter(p, "dp", scatter_dimension=0, tiled=True) for p in parts]
    deltas = elementwise(*sums)
    hidden, gate_delta, up_delta = [lax.all_gather(d, "dp", axis=0, tiled=True) for d in deltas]
    partial_input = contract_last(gate_delta, gate_weight) + contract_last(up_delta, up_weight)
    parts = partial_input.reshape(8, -1, width)
    input_grad = jnp.sum(lax.all_to_all(parts, "blk", 0, 0, tiled=True), axis=0)
    down_grad = contract_first(hidden, grads_all).astype(jnp.bfloat16)
    gate_grad = contract_first(rows_all, gate_delta).astype(jnp.bfloat16)
    up_grad = contract_first(rows_all, up_delta).astype(jnp.bfloat16)
    return (input_grad.astype(jnp.bfloat16), gate_grad, up_grad, down_grad)


def solution(mesh):
    return jax.shard_map(
        local,
        mesh=mesh,
        in_specs=(P("blk", "dp"), P("blk", "dp"), P("dp", "blk"), P("dp", "blk"), P("blk", "dp")),
        out_specs=(P("blk", "dp"), P("dp", "blk"), P("dp", "blk"), P("blk", "dp")),
        check_vma=False,
    )
```

profile of v0, /device:TPU:1, one launch (start us, length us, event | category | flops | bytes accessed | tf_op | source)
XLA Modules:
  0.0 462.0 jit_solution(15373133980176718704)
XLA Ops:
  7.2 0.0 copy-start
  7.2 0.0 all-gather.5.cloned.1.call-start
  7.2 1.7 pad_maximum_fusion
  8.9 0.0 all-gather.5.cloned.1.call-update
  8.9 0.0 reduce-scatter.4.cloned.1.call-start
  9.0 39.6 %all-gather.5.cloned.1.call-done = bf16[512,1024]{1,0:T(8,128)(2,1)} async-done(((bf16[64,1024]{1,0:T(8,128)(2,1)}), bf16[512,1024]{1,0:T(8,128)(2,1)}) %all-gather.5.cloned.1.call-update) | async-done | bytes 1048592 | tf_op jit(solution)/shard_map/all_gather | solution.py:28
  48.6 4.8 %fusion.1 = f32[512,1848]{1,0:T(8,128)} fusion(bf16[1848,512]{1,0:T(8,128)(2,1)} %param.9, bf16[512,1024]{1,0:T(8,128)(2,1)} %all-gather.5.cloned.1.call-done), kind=kOutput, calls=%fused_computation.5 | convolution fusion | flops 968884224 | bytes 6201344 | tf_op jit(solution)/shard_map/dot_general | solution.py:8
  53.4 0.0 copy-start.1
  53.4 0.0 reduce-scatter.4.cloned.1.call-update
  53.5 0.0 reduce-scatter.6.cloned.1.call-start
  53.5 1.1 copy-done.1
  54.7 4.7 %fusion.7 = f32[512,1848]{1,0:T(8,128)} fusion(bf16[512,1848]{0,1:T(8,128)(2,1)} %param.8, bf16[512,1024]{1,0:T(8,128)(2,1)S(1)} %copy-done.1), kind=kOutput, calls=%fused_computation.11 | convolution fusion | flops 968884224 | bytes 6201344 | tf_op jit(solution)/shard_map/dot_general | solution.py:33
  59.3 0.0 reduce-scatter.6.cloned.1.call-update
  59.4 0.0 reduce-scatter.8.cloned.1.call-start
  59.4 0.0 copy-done
  59.4 3.3 fusion.5
  62.7 0.0 reduce-scatter.8.cloned.1.call-update
  62.7 0.0 all-gather.7.cloned.1.call-start
  62.7 72.9 %reduce-scatter.4.cloned.1.call-done = f32[32,1848]{1,0:T(8,128)} async-done(((f32[512,1848]{1,0:T(8,128)}), f32[32,1848]{1,0:T(8,128)}) %reduce-scatter.4.cloned.1.call-update) | async-done | bytes 236560 | tf_op jit(solution)/shard_map/reduce_scatter | solution.py:36
  135.7 81.9 %reduce-scatter.6.cloned.1.call-done = f32[32,1848]{1,0:T(8,128)} async-done(((f32[512,1848]{1,0:T(8,128)}), f32[32,1848]{1,0:T(8,128)}) %reduce-scatter.6.cloned.1.call-update) | async-done | bytes 236560 | tf_op jit(solution)/shard_map/reduce_scatter | solution.py:36
  217.6 81.8 %reduce-scatter.8.cloned.1.call-done = f32[32,1848]{1,0:T(8,128)} async-done(((f32[512,1848]{1,0:T(8,128)}), f32[32,1848]{1,0:T(8,128)}) %reduce-scatter.8.cloned.1.call-update) | async-done | bytes 236560 | tf_op jit(solution)/shard_map/reduce_scatter | solution.py:36
  299.4 2.0 multiply_convert_fusion
  301.5 0.0 all-gather.7.cloned.1.call-update
  301.5 0.0 all-gather.9.cloned.1.call-start
  301.5 0.5 all-gather.9.cloned.1.call-update
  302.1 0.0 all-gather.11.cloned.1.call-start
  302.1 0.7 all-gather.11.cloned.1.call-update
  302.8 47.4 %all-gather.7.cloned.1.call-done = bf16[512,1848]{1,0:T(8,128)(2,1)} async-done(((bf16[32,1848]{1,0:T(8,128)(2,1)}), bf16[512,1848]{1,0:T(8,128)(2,1)}) %all-gather.7.cloned.1.call-update) | async-done | bytes 1892368 | tf_op jit(solution)/shard_map/all_gather | solution.py:38
  350.2 3.8 fusion.9
  354.0 45.2 %all-gather.9.cloned.1.call-done = bf16[512,1848]{1,0:T(8,128)(2,1)} async-done(((bf16[32,1848]{1,0:T(8,128)(2,1)}), bf16[512,1848]{1,0:T(8,128)(2,1)}) %all-gather.9.cloned.1.call-update) | async-done | bytes 1892368 | tf_op jit(solution)/shard_map/all_gather | solution.py:38
  399.2 4.6 convolution_add_fusion
  403.8 4.2 all-to-all-start
  408.0 0.0 copy-start.2
  408.0 4.2 convolution_convert_fusion.1
  412.2 0.0 copy-done.2
  412.2 2.4 convolution_convert_fusion.2
  414.6 34.6 %all-gather.11.cloned.1.call-done = bf16[512,1848]{1,0:T(8,128)(2,1)} async-done(((bf16[32,1848]{1,0:T(8,128)(2,1)}), bf16[512,1848]{1,0:T(8,128)(2,1)}) %all-gather.11.cloned.1.call-update) | async-done | bytes 1892368 | tf_op jit(solution)/shard_map/all_gather | solution.py:38
  449.2 4.0 convolution_convert_fusion
  453.2 0.0 all-to-all-done
  453.2 1.9 reduce_sum.9
Async XLA Ops:
  7.2 52.2 %copy-start = (bf16[512,1848]{0,1:T(8,128)(2,1)S(1)}, bf16[512,1848]{0,1:T(8,128)(2,1)}, u32[]{:S(2)}) copy-start(bf16[512,1848]{0,1:T(8,128)(2,1)} %param.7) | copy-start | bytes 5677060
  7.2 41.4 %all-gather.5.cloned.1.call-start = ((), (), s32[]{:S(2)}) async-start(), calls=%async_computation.4 | async-start | bytes 1179648 | tf_op jit(solution)/shard_map/all_gather | solution.py:28
  8.9 126.8 %reduce-scatter.4.cloned.1.call-start = ((), (), s32[]{:S(2)}) async-start(), calls=%async_computation.5 | async-start | bytes 4177920 | tf_op jit(solution)/shard_map/reduce_scatter | solution.py:36
  53.4 1.2 copy-start.1
  53.5 164.2 %reduce-scatter.6.cloned.1.call-start = ((), (), s32[]{:S(2)}) async-start(), calls=%async_computation.6 | async-start | bytes 4177920 | tf_op jit(solution)/shard_map/reduce_scatter | solution.py:36
  59.4 240.1 %reduce-scatter.8.cloned.1.call-start = ((), (), s32[]{:S(2)}) async-start(), calls=%async_computation.7 | async-start | bytes 4177920 | tf_op jit(solution)/shard_map/reduce_scatter | solution.py:36
  62.7 287.5 %all-gather.7.cloned.1.call-start = ((), (), s32[]{:S(2)}) async-start(), calls=%async_computation.8 | async-start | bytes 2088960 | tf_op jit(solution)/shard_map/all_gather | solution.py:38
  301.5 97.7 %all-gather.9.cloned.1.call-start = ((), (), s32[]{:S(2)}) async-start(), calls=%async_computation.9 | async-start | bytes 2088960 | tf_op jit(solution)/shard_map/all_gather | solution.py:38
  302.1 147.1 %all-gather.11.cloned.1.call-start = ((), (), s32[]{:S(2)}) async-start(), calls=%async_computation.10 | async-start | bytes 2088960 | tf_op jit(solution)/shard_map/all_gather | solution.py:38
  403.8 49.4 %all-to-all-start = ((f32[8,64,512]{2,1,0:T(8,128)}), f32[8,64,512]{2,1,0:T(8,128)}, u32[]{:S(2)}, u32[]{:S(2)}) async-start(f32[8,64,512]{2,1,0:T(8,128)} %bitcast.11), calls=%async_computation.3 | async-start | bytes 2097152 | tf_op jit(solution)/shard_map/all_to_all | solution.py:41
  408.0 4.2 copy-start.2
Sparse Core Ops, SparseCore 0:
  10.2 38.3 all-gather.4
  53.6 82.0 reduce-scatter.3
  139.8 77.7 reduce-scatter.5
  221.6 77.7 reduce-scatter.7
  302.3 47.8 all-gather.6
  353.1 46.0 all-gather.8
  401.7 47.4 all-gather.10
where the time goes:
time: 462 us
  waiting for transfers between devices  405 us (88%)
  matrix products  31.7 us (7%)
  between operations  14.2 us (3%)
  other arithmetic  5.63 us (1%)
    reduce_scatter x3, waiting for transfers between devices, local(): lax.psum_scatter(p, 'dp', scatter_dimension=0, tiled=True)  237 us
    all_gather x3, waiting for transfers between devices, local(): lax.all_gather(d, 'dp', axis=0, tiled=True)  127 us
    all_gather x1, waiting for transfers between devices, local(): lax.all_gather(jnp.concatenate([inputs, upstream], 1), 'blk', axis=0, til...  39.6 us
    dot_general x3, matrix products, contract_last(): lax.dot_general(left, right, (((1,), (1,)), ((), ())), preferred_element_...  13.2 us
    dot_general x3, matrix products, contract_first(): lax.dot_general(left, right, (((0,), (0,)), ((), ())), preferred_element_...  10.6 us
  transfers between devices with their start and end apart: 8, of which 7 were waited for; matrix products, arithmetic and copies ran while one was open for 6% of the time, Pallas kernels for 0%

commit v1 on v0

--- a/solution.py
+++ b/solution.py
@@ -35,7 +35,10 @@
     ]
     sums = [lax.psum_scatter(p, "dp", scatter_dimension=0, tiled=True) for p in parts]
     deltas = elementwise(*sums)
-    hidden, gate_delta, up_delta = [lax.all_gather(d, "dp", axis=0, tiled=True) for d in deltas]
+    hidden, gate_delta, up_delta = [
+        jnp.concatenate(lax.all_to_all(jnp.stack([d] * lax.axis_size("dp")), "dp", 0, 0), axis=0)
+        for d in deltas
+    ]
     partial_input = contract_last(gate_delta, gate_weight) + contract_last(up_delta, up_weight)
     parts = partial_input.reshape(8, -1, width)
     input_grad = jnp.sum(lax.all_to_all(parts, "blk", 0, 0, tiled=True), axis=0)

time: 462 us -> 429 us (0.929)
  waiting for transfers between devices: 405 us -> 302 us
  blocking collectives: 0 us -> 63.6 us
  starting transfers between devices: 4.53 us -> 10.7 us
    all_gather x3 -> x0, waiting for transfers between devices: 127 us -> none  [local(): lax.all_gather(d, 'dp', axis=0, tiled=True)]
    all_to_all x0 -> x2, blocking collectives: none -> 63.6 us  [local(): lax.all_to_all(jnp.stack([d] * lax.axis_size('dp')), 'dp', 0, 0)]
    all_to_all x0 -> x1, waiting for transfers between devices: none -> 21.8 us  [local(): lax.all_to_all(jnp.stack([d] * lax.axis_size('dp')), 'dp', 0, 0)]
    all_to_all x0 -> x1, starting transfers between devices: none -> 5.42 us  [local(): lax.all_to_all(jnp.stack([d] * lax.axis_size('dp')), 'dp', 0, 0)]
  transfers between devices with their start and end apart: 8 -> 6, of which waited for: 7 -> 6; matrix products, arithmetic and copies ran while one was open for 6% -> 6% of each run, Pallas kernels for 0% -> 0%
where the time goes in v1:
time: 429 us; the launch traced here: 427 us
  waiting for transfers between devices  302 us (70%)
  blocking collectives  63.6 us (15%)
  matrix products  28.6 us (7%)
  between operations  13.8 us (3%)
  starting transfers between devices  10.7 us (2%)
  other arithmetic  4.93 us (1%)
    reduce_scatter x3, waiting for transfers between devices, local(): lax.psum_scatter(p, 'dp', scatter_dimension=0, tiled=True)  237 us
    all_to_all x2, blocking collectives, local(): lax.all_to_all(jnp.stack([d] * lax.axis_size('dp')), 'dp', 0, 0)  63.6 us
    all_gather x1, waiting for transfers between devices, local(): lax.all_gather(jnp.concatenate([inputs, upstream], 1), 'blk', axis=0, til...  39.6 us
    all_to_all x1, waiting for transfers between devices, local(): lax.all_to_all(jnp.stack([d] * lax.axis_size('dp')), 'dp', 0, 0)  21.8 us
    dot_general x3, matrix products, contract_first(): lax.dot_general(left, right, (((0,), (0,)), ((), ())), preferred_element_...  10.6 us
    dot_general x3, matrix products, contract_last(): lax.dot_general(left, right, (((1,), (1,)), ((), ())), preferred_element_...  10.1 us
  transfers between devices with their start and end apart: 6, of which 6 were waited for; matrix products, arithmetic and copies ran while one was open for 6% of the time, Pallas kernels for 0%

profile of v1, /device:TPU:1, one launch (start us, length us, event | category | flops | bytes accessed | tf_op | source)
XLA Modules:
  0.0 426.5 jit_solution(295176259943262406)
XLA Ops:
  7.2 0.0 copy-start
  7.2 0.0 all-gather.2.cloned.1.call-start
  7.2 1.7 pad_maximum_fusion
  8.9 0.0 all-gather.2.cloned.1.call-update
  8.9 0.0 reduce-scatter.4.cloned.1.call-start
  9.0 39.6 %all-gather.2.cloned.1.call-done = bf16[512,1024]{1,0:T(8,128)(2,1)} async-done(((bf16[64,1024]{1,0:T(8,128)(2,1)}), bf16[512,1024]{1,0:T(8,128)(2,1)}) %all-gather.2.cloned.1.call-update) | async-done | bytes 1048592 | tf_op jit(solution)/shard_map/all_gather | solution.py:28
  48.6 4.8 %fusion.1 = f32[512,1848]{1,0:T(8,128)} fusion(bf16[1848,512]{1,0:T(8,128)(2,1)} %param.9, bf16[512,1024]{1,0:T(8,128)(2,1)} %all-gather.2.cloned.1.call-done), kind=kOutput, calls=%fused_computation.5 | convolution fusion | flops 968884224 | bytes 6201344 | tf_op jit(solution)/shard_map/dot_general | solution.py:8
  53.5 0.0 copy-start.1
  53.5 0.0 reduce-scatter.4.cloned.1.call-update
  53.5 0.0 reduce-scatter.6.cloned.1.call-start
  53.5 1.1 copy-done.1
  54.7 4.7 %fusion.7 = f32[512,1848]{1,0:T(8,128)} fusion(bf16[512,1848]{0,1:T(8,128)(2,1)} %param.8, bf16[512,1024]{1,0:T(8,128)(2,1)S(1)} %copy-done.1), kind=kOutput, calls=%fused_computation.11 | convolution fusion | flops 968884224 | bytes 6201344 | tf_op jit(solution)/shard_map/dot_general | solution.py:33
  59.4 0.0 reduce-scatter.6.cloned.1.call-update
  59.4 0.0 reduce-scatter.8.cloned.1.call-start
  59.5 0.0 copy-done
  59.5 3.3 fusion.5
  62.7 0.0 reduce-scatter.8.cloned.1.call-update
  62.8 73.0 %reduce-scatter.4.cloned.1.call-done = f32[32,1848]{1,0:T(8,128)} async-done(((f32[512,1848]{1,0:T(8,128)}), f32[32,1848]{1,0:T(8,128)}) %reduce-scatter.4.cloned.1.call-update) | async-done | bytes 236560 | tf_op jit(solution)/shard_map/reduce_scatter | solution.py:36
  135.7 81.9 %reduce-scatter.6.cloned.1.call-done = f32[32,1848]{1,0:T(8,128)} async-done(((f32[512,1848]{1,0:T(8,128)}), f32[32,1848]{1,0:T(8,128)}) %reduce-scatter.6.cloned.1.call-update) | async-done | bytes 236560 | tf_op jit(solution)/shard_map/reduce_scatter | solution.py:36
  217.6 81.8 %reduce-scatter.8.cloned.1.call-done = f32[32,1848]{1,0:T(8,128)} async-done(((f32[512,1848]{1,0:T(8,128)}), f32[32,1848]{1,0:T(8,128)}) %reduce-scatter.8.cloned.1.call-update) | async-done | bytes 236560 | tf_op jit(solution)/shard_map/reduce_scatter | solution.py:36
  299.5 1.3 multiply_convert_fusion
  300.8 0.1 stack.6
  300.9 32.5 %all_to_all.20 = bf16[16,32,1848]{2,1,0:T(8,128)(2,1)} all-to-all(bf16[16,32,1848]{2,1,0:T(8,128)(2,1)S(1)} %stack.6), channel_id=1, replica_groups=mesh['dp'=16,'blk'=8] {'dp'}, dimensions={0} | all-to-all | bytes 3784704 | tf_op jit(solution)/shard_map/all_to_all | solution.py:39
  333.4 0.1 stack.7
  333.5 31.1 %all_to_all.21 = bf16[16,32,1848]{2,1,0:T(8,128)(2,1)} all-to-all(bf16[16,32,1848]{2,1,0:T(8,128)(2,1)S(1)} %stack.7), channel_id=1, replica_groups=mesh['dp'=16,'blk'=8] {'dp'}, dimensions={0} | all-to-all | bytes 3784704 | tf_op jit(solution)/shard_map/all_to_all | solution.py:39
  364.6 1.4 stack.8
  366.1 5.4 %all-to-all-start.3 = ((bf16[16,32,1848]{2,1,0:T(8,128)(2,1)}), bf16[16,32,1848]{2,1,0:T(8,128)(2,1)}, u32[]{:S(2)}, u32[]{:S(2)}) async-start(bf16[16,32,1848]{2,1,0:T(8,128)(2,1)} %stack.8), calls=%async_computation.6 | async-start | bytes 3932160 | tf_op jit(solution)/shard_map/all_to_all | solution.py:39
  371.5 0.0 copy-start.3
  371.5 0.0 copy-start.4
  371.5 2.9 fusion.9
  374.5 0.0 copy-done.3
  374.5 0.0 copy-done.4
  374.5 2.3 convolution_add_fusion
  376.8 21.8 %all-to-all-done.3 = bf16[16,32,1848]{2,1,0:T(8,128)(2,1)} async-done(((bf16[16,32,1848]{2,1,0:T(8,128)(2,1)}), bf16[16,32,1848]{2,1,0:T(8,128)(2,1)}, u32[]{:S(2)}, u32[]{:S(2)}) %all-to-all-start.3) | async-done | bytes 1892384 | tf_op jit(solution)/shard_map/all_to_all | solution.py:39
  398.6 5.1 %all-to-all-start.2 = ((f32[8,64,512]{2,1,0:T(8,128)}), f32[8,64,512]{2,1,0:T(8,128)}, u32[]{:S(2)}, u32[]{:S(2)}) async-start(f32[8,64,512]{2,1,0:T(8,128)} %bitcast.18), calls=%async_computation.5 | async-start | bytes 2097152 | tf_op jit(solution)/shard_map/all_to_all | solution.py:44
  403.8 0.0 copy-start.2
  403.8 4.1 convolution_convert_fusion.1
  407.9 0.0 copy-done.2
  407.9 2.5 convolution_convert_fusion.2
  410.4 4.0 convolution_convert_fusion
  414.3 3.7 all-to-all-done.2
  418.1 1.9 reduce_sum.9
Async XLA Ops:
  7.2 52.3 %copy-start = (bf16[512,1848]{0,1:T(8,128)(2,1)S(1)}, bf16[512,1848]{0,1:T(8,128)(2,1)}, u32[]{:S(2)}) copy-start(bf16[512,1848]{0,1:T(8,128)(2,1)} %param.7) | copy-start | bytes 5677060
  7.2 41.4 %all-gather.2.cloned.1.call-start = ((), (), s32[]{:S(2)}) async-start(), calls=%async_computation.7 | async-start | bytes 1179648 | tf_op jit(solution)/shard_map/all_gather | solution.py:28
  8.9 126.8 %reduce-scatter.4.cloned.1.call-start = ((), (), s32[]{:S(2)}) async-start(), calls=%async_computation.8 | async-start | bytes 4177920 | tf_op jit(solution)/shard_map/reduce_scatter | solution.py:36
  53.5 1.2 copy-start.1
  53.5 164.2 %reduce-scatter.6.cloned.1.call-start = ((), (), s32[]{:S(2)}) async-start(), calls=%async_computation.9 | async-start | bytes 4177920 | tf_op jit(solution)/shard_map/reduce_scatter | solution.py:36
  59.4 240.1 %reduce-scatter.8.cloned.1.call-start = ((), (), s32[]{:S(2)}) async-start(), calls=%async_computation.10 | async-start | bytes 4177920 | tf_op jit(solution)/shard_map/reduce_scatter | solution.py:36
  366.1 32.6 %all-to-all-start.3 = ((bf16[16,32,1848]{2,1,0:T(8,128)(2,1)}), bf16[16,32,1848]{2,1,0:T(8,128)(2,1)}, u32[]{:S(2)}, u32[]{:S(2)}) async-start(bf16[16,32,1848]{2,1,0:T(8,128)(2,1)} %stack.8), calls=%async_computation.6 | async-start | bytes 3932160 | tf_op jit(solution)/shard_map/all_to_all | solution.py:39
  371.5 3.0 copy-start.3
  371.5 3.0 copy-start.4
  398.6 19.4 %all-to-all-start.2 = ((f32[8,64,512]{2,1,0:T(8,128)}), f32[8,64,512]{2,1,0:T(8,128)}, u32[]{:S(2)}, u32[]{:S(2)}) async-start(f32[8,64,512]{2,1,0:T(8,128)} %bitcast.18), calls=%async_computation.5 | async-start | bytes 2097152 | tf_op jit(solution)/shard_map/all_to_all | solution.py:44
  403.8 4.1 copy-start.2
Sparse Core Ops, SparseCore 0:
  10.2 38.3 all-gather.1
  53.6 82.0 reduce-scatter.3
  139.9 77.7 reduce-scatter.5
  221.6 77.7 reduce-scatter.7
